TPU v7x, 32 devices: a whole 2x2x4 slice. The times are simulated.
32 devices in a mesh: group: 4 (over z), seq: 4 (over y, core), mp: 2 (over x).
Axes of the slice: x: 2, y: 2, z: 4, core: 2. Of those that a mesh axis runs over, the one named last changes fastest.
Arguments:
- patches: bfloat16 [8192, 640], P(('group', 'seq')), may hold values from -6 to 6
- w_merge1: bfloat16 [4, 640, 2560], P(None, 'seq', 'mp'), may hold values from -0.125 to 0.125
- w_merge2: bfloat16 [2560, 4096], P('mp', 'seq'), may hold values from -0.125 to 0.125
- w_query: bfloat16 [4096, 4096], P('seq', 'mp'), may hold values from -0.09375 to 0.09375
- w_keyval: bfloat16 [4096, 2, 1024], P('seq', None, 'mp'), may hold values from -0.09375 to 0.09375
- attn_grad: bfloat16 [2048, 4096], P(('group', 'seq'), 'mp'), may hold values from -6 to 6
- sample_ids: int32 [4, 512], P('group'), may hold values from 0 to 7, never falling along the last dimension, each value on 1 to 384 neighbouring positions
Outputs:
- patch_grad: bfloat16 [8192, 640], P(('group', 'seq', 'mp'))
Inputs may be any that keep to these rules, and one draw needn't show every extreme that they name: `sample_ids`: in each sequence never falls; every sample spans 1 to 384 tokens.
All inputs are finite; a program needn't handle non-finite values.
Results may differ from a plain program's by a relative error of at most 0.035.
Values may be sent and summed in bfloat16 or wider, within the bound.
No kernel may reach another device: no remote copies, remote signals or barrier semaphores. Data moves between devices by JAX's collectives and lax.ppermute only.
A program may use at most 128 MiB of HBM per device.

v0:
```python
import jax
import jax.numpy as jnp
from jax import lax
from jax.sharding import PartitionSpec as P

HEAD = 128
EPSILON = 1e-06
NEGATIVE = 1e30


def shifted_2(value, axis, steps):
    count = lax.axis_size(axis)
    initial, last = (max(0, -steps), min(count, count - steps))
    return lax.ppermute(value, axis, [(source, source + steps) for source in range(initial, last)])


def gelu_grad(inputs):
    normal_cdf = 0.5 * (1.0 + lax.erf(inputs * 0.7071067811865476))
    normal_pdf = jnp.exp(-0.5 * inputs * inputs) * 0.3989422804014327
    return normal_cdf + inputs * normal_pdf


def fetch_earlier(own_keyval, offset):
    return shifted_2(own_keyval, "seq", offset)


def return_terms(terms, offset):
    return (
        shifted_2(terms[0].astype(jnp.bfloat16), "seq", -offset).astype(jnp.float32),
        shifted_2(terms[1].astype(jnp.bfloat16), "seq", -offset).astype(jnp.float32),
    )


def local(patches, w_merge1, w_merge2, w_query, w_keyval, attn_grad, sample_ids):
    patch_rows, feat_width = patches.shape
    tok_rows = patch_rows // 4
    score_scale = HEAD ** (-0.5)
    values = patches.astype(jnp.float32)
    row_mean = jnp.mean(values, -1, keepdims=True)
    ln_scale = lax.rsqrt(
        jnp.mean(values * values, -1, keepdims=True) - row_mean * row_mean + EPSILON
    )
    normed = (values - row_mean) * ln_scale
    merge_in = normed.astype(jnp.bfloat16).reshape(tok_rows, 4 * feat_width)
    first_tile = lax.all_gather(w_merge1, "seq", axis=1, tiled=True)
    first_flat = first_tile.reshape(4 * feat_width, first_tile.shape[2])
    hidden_pre = jnp.dot(merge_in, first_flat, preferred_element_type=jnp.float32)
    hidden = jax.nn.gelu(hidden_pre, approximate=False).astype(jnp.bfloat16)
    second_tile = lax.all_gather(w_merge2, "seq", axis=1, tiled=True)
    model_width = second_tile.shape[1]
    partial_value = jnp.dot(hidden, second_tile, preferred_element_type=jnp.float32)
    merged = lax.psum(partial_value.astype(jnp.bfloat16), "mp")
    merged_f = merged.astype(jnp.float32)
    rms_scale = lax.rsqrt(jnp.mean(merged_f * merged_f, -1, keepdims=True) + EPSILON)
    normed_tok = merged_f * rms_scale
    query_tile, keyval_tile = (
        lax.all_gather(w_query, "seq", axis=0, tiled=True),
        lax.all_gather(w_keyval, "seq", axis=0, tiled=True),
    )
    kv_part = keyval_tile.shape[2]
    keyval_flat = keyval_tile.reshape(model_width, 2 * kv_part)
    normed_bf = normed_tok.astype(jnp.bfloat16)
    queries = jnp.dot(normed_bf, query_tile, preferred_element_type=jnp.float32).astype(
        jnp.bfloat16
    )
    own_keyval = jnp.dot(normed_bf, keyval_flat, preferred_element_type=jnp.float32).astype(
        jnp.bfloat16
    )
    query_part = queries.shape[1]
    kv_local = kv_part // HEAD
    per_kv = query_part // HEAD // kv_local
    run_ids = sample_ids[0]
    run_len = run_ids.shape[0]
    own_start = lax.axis_index("seq") * tok_rows
    reach = min(lax.axis_size("seq") - 1, (run_len // 2 + 2 * tok_rows - 2) // tok_rows)
    pieces = [own_keyval]
    for offset in range(1, reach + 1):
        pieces.insert(0, fetch_earlier(own_keyval, offset))
    window_kv = jnp.concatenate(pieces, 0)
    window_rows = window_kv.shape[0]
    key_pos = own_start - reach * tok_rows + jnp.arange(window_rows, dtype=jnp.int32)
    padded_ids = jnp.concatenate([jnp.full((reach * tok_rows,), -1, jnp.int32), run_ids], 0)
    key_ids = lax.dynamic_slice_in_dim(padded_ids, own_start, window_rows, 0)
    total_rows = window_kv.shape[0]
    key_heads = window_kv[:, :kv_part].reshape(total_rows, kv_local, HEAD)
    value_heads = window_kv[:, kv_part:].reshape(total_rows, kv_local, HEAD)
    query_pos = own_start + jnp.arange(tok_rows, dtype=jnp.int32)
    own_ids = lax.dynamic_slice_in_dim(run_ids, own_start, tok_rows, 0)
    allowed = (query_pos[:, None] >= key_pos[None, :]) & (own_ids[:, None] == key_ids[None, :])
    query_heads = queries.reshape(tok_rows, kv_local, per_kv, HEAD)
    scores = (
        jnp.einsum("tkgd,ukd->kgtu", query_heads, key_heads, preferred_element_type=jnp.float32)
        * score_scale
    )
    scores = jnp.where(allowed, scores, -NEGATIVE)
    row_max = jnp.max(scores, -1, keepdims=True)
    shifted = jnp.exp(scores - row_max)
    soft = shifted / jnp.sum(shifted, -1, keepdims=True)
    soft_bf = soft.astype(jnp.bfloat16)
    attended = jnp.einsum(
        "kgtu,ukd->tkgd", soft_bf, value_heads, preferred_element_type=jnp.float32
    )
    grad_heads = attn_grad.reshape(tok_rows, kv_local, per_kv, HEAD)
    row_delta = jnp.sum(grad_heads.astype(jnp.float32) * attended, -1)
    dprob = jnp.einsum(
        "tkgd,ukd->kgtu", grad_heads, value_heads, preferred_element_type=jnp.float32
    )
    dscore = (soft * (dprob - jnp.transpose(row_delta, (1, 2, 0))[..., None])).astype(jnp.bfloat16)
    dquery = (
        jnp.einsum("kgtu,ukd->tkgd", dscore, key_heads, preferred_element_type=jnp.float32)
        * score_scale
    )
    dquery = dquery.astype(jnp.bfloat16).reshape(tok_rows, query_part)
    dkey_terms = (
        jnp.einsum("kgtu,tkgd->ukd", dscore, query_heads, preferred_element_type=jnp.float32)
        * score_scale
    )
    dvalue_terms = jnp.einsum(
        "kgtu,tkgd->ukd", soft_bf, grad_heads, preferred_element_type=jnp.float32
    )
    dkey = dkey_terms[reach * tok_rows :]
    dvalue = dvalue_terms[reach * tok_rows :]
    for offset in range(1, reach + 1):
        begin_row = (reach - offset) * tok_rows
        key_back, value_back = return_terms(
            (
                dkey_terms[begin_row : begin_row + tok_rows],
                dvalue_terms[begin_row : begin_row + tok_rows],
            ),
            offset,
        )
        dkey = dkey + key_back
        dvalue = dvalue + value_back
    grads_kv = jnp.concatenate(
        [
            dkey.astype(jnp.bfloat16).reshape(tok_rows, kv_part),
            dvalue.astype(jnp.bfloat16).reshape(tok_rows, kv_part),
        ],
        1,
    )
    dnormed_part = jnp.einsum("tc,dc->td", dquery, query_tile, preferred_element_type=jnp.float32)
    dnormed_part = dnormed_part + jnp.einsum(
        "tc,dc->td", grads_kv, keyval_flat, preferred_element_type=jnp.float32
    )
    dnormed = lax.psum(dnormed_part.astype(jnp.bfloat16), "mp").astype(jnp.float32)
    inner_mean = jnp.mean(dnormed * normed_tok, -1, keepdims=True)
    dmerged = (rms_scale * (dnormed - normed_tok * inner_mean)).astype(jnp.bfloat16)
    dhidden = jnp.einsum("td,hd->th", dmerged, second_tile, preferred_element_type=jnp.float32)
    dhidden_pre = (dhidden * gelu_grad(hidden_pre)).astype(jnp.bfloat16)
    dmerge_part = jnp.einsum(
        "th,fh->tf", dhidden_pre, first_flat, preferred_element_type=jnp.float32
    )
    dmerge_in = lax.psum_scatter(
        dmerge_part.reshape(patch_rows, feat_width).astype(jnp.bfloat16),
        "mp",
        scatter_dimension=0,
        tiled=True,
    ).astype(jnp.float32)
    share_rows = dmerge_in.shape[0]
    begin = lax.axis_index("mp") * share_rows
    own_normed = lax.dynamic_slice_in_dim(normed, begin, share_rows, 0)
    own_scale = lax.dynamic_slice_in_dim(ln_scale, begin, share_rows, 0)
    first_mean = jnp.mean(dmerge_in, -1, keepdims=True)
    second_mean = jnp.mean(dmerge_in * own_normed, -1, keepdims=True)
    patch_grad = own_scale * (dmerge_in - first_mean - own_normed * second_mean)
    return patch_grad.astype(jnp.bfloat16)


def solution(mesh):
    in_specs = (
        P(("group", "seq"), None),
        P(None, "seq", "mp"),
        P("mp", "seq"),
        P("seq", "mp"),
        P("seq", None, "mp"),
        P(("group", "seq"), "mp"),
        P("group", None),
    )
    out_specs = P(("group", "seq", "mp"), None)
    return jax.shard_map(local, mesh=mesh, in_specs=in_specs, out_specs=out_specs, check_vma=False)
```

profile of v0, /device:TPU:0, one launch (start us, length us, event | category | flops | bytes accessed | tf_op | source)
XLA Modules:
  0.0 488.3 jit_solution(8009914416394618098)
XLA Ops:
  6.5 0.7 all-gather.5.cloned.1.call-update
  7.3 0.7 all-gather.7.cloned.1.call-update
  8.1 0.7 all-gather.9.cloned.1.call-update
  8.8 0.3 convert_reduce_fusion
  9.1 1.4 fusion.20
  10.4 0.4 reshape.109
  10.8 48.7 %all-gather.5.cloned.1.call-done = bf16[4,640,1280]{2,1,0:T(8,128)(2,1)} async-done(((bf16[4,160,1280]{2,1,0:T(8,128)(2,1)}), bf16[4,640,1280]{2,1,0:T(8,128)(2,1)}) %all-gather.5.cloned.1.call-update) | async-done | bytes 6553616 | tf_op jit(solution)/shard_map/all_gather | solution.py:45
  59.5 3.9 fusion.140
  63.4 67.9 %all-gather.7.cloned.1.call-done = bf16[1280,4096]{1,0:T(8,128)(2,1)} async-done(((bf16[1280,1024]{1,0:T(8,128)(2,1)}), bf16[1280,4096]{1,0:T(8,128)(2,1)}) %all-gather.7.cloned.1.call-update) | async-done | bytes 10485776 | tf_op jit(solution)/shard_map/all_gather | solution.py:49
  131.3 7.8 %convolution_convert_fusion = bf16[128,4096]{1,0:T(8,128)(2,1)} fusion(bf16[1280,4096]{1,0:T(8,128)(2,1)} %all-gather.7.cloned.1.call-done, f32[128,1280]{1,0:T(8,128)S(1)} %fusion.140), kind=kOutput, calls=%fused_computation.3 | convolution fusion | flops 1353351168 | bytes 12189696 | tf_op jit(solution)/shard_map/dot_general | solution.py:51
  139.1 0.0 all-gather.11.cloned.1.call-start
  139.1 0.5 all-gather.11.cloned.1.call-update
  139.8 0.1 pad_dynamic-slice_fusion
  139.9 51.3 %all-gather.9.cloned.1.call-done = bf16[4096,2,512]{2,1,0:T(2,128)(2,1)} async-done(((bf16[1024,2,512]{2,1,0:T(2,128)(2,1)}), bf16[4096,2,512]{2,1,0:T(2,128)(2,1)}) %all-gather.9.cloned.1.call-update) | async-done | bytes 8388624 | tf_op jit(solution)/shard_map/all_gather | solution.py:58
  191.1 9.3 %copy.52 = bf16[512,8,2,512]{3,1,2,0:T(8,128)(2,1)} copy(bf16[512,8,2,512]{3,2,1,0:T(2,128)(2,1)} %bitcast.81) | data formatting | bytes 16777216
  200.5 33.0 %all-reduce.4.cloned.1.call-done = bf16[128,4096]{1,0:T(8,128)(2,1)} async-done(((bf16[128,4096]{1,0:T(8,128)(2,1)}), bf16[128,4096]{1,0:T(8,128)(2,1)}) %all-reduce.4.cloned.1.call-update) | async-done | bytes 1048592 | tf_op jit(solution)/shard_map/psum | solution.py:52
  233.5 1.5 fusion.8
  235.0 5.1 %convolution_convert_fusion.3 = bf16[128,1024]{1,0:T(8,128)(2,1)S(1)} fusion(bf16[4096,1024]{1,0:T(8,128)(2,1)} %bitcast.79, bf16[128,4096]{1,0:T(8,128)(2,1)} %all-reduce.4.cloned.1.call-done, f32[128]{0:T(128)S(1)} %add_rsqrt_fusion.1), kind=kOutput, calls=%fused_computation.43 | convolution fusion | flops 1075445760 | bytes 9699840 | tf_op jit(solution)/shard_map/dot_general | solution.py:66
  240.1 1.6 collective-permute-start.2
  241.7 3.7 collective-permute-start.1
  245.4 1.5 collective-permute-start
  246.9 0.3 copy.22
  247.2 0.2 compare_and_fusion
  247.4 10.1 %collective-permute-done.1 = bf16[128,1024]{1,0:T(8,128)(2,1)S(1)} collective-permute-done((bf16[128,1024]{1,0:T(8,128)(2,1)S(1)}, bf16[128,1024]{1,0:T(8,128)(2,1)S(1)}, u32[]{:S(2)}, u32[]{:S(2)}) %collective-permute-start.1) | collective-permute-done | bytes 262176 | tf_op jit(solution)/shard_map/ppermute | solution.py:14
  257.5 8.7 %collective-permute-done = bf16[128,1024]{1,0:T(8,128)(2,1)S(1)} collective-permute-done((bf16[128,1024]{1,0:T(8,128)(2,1)S(1)}, bf16[128,1024]{1,0:T(8,128)(2,1)S(1)}, u32[]{:S(2)}, u32[]{:S(2)}) %collective-permute-start) | collective-permute-done | bytes 262176 | tf_op jit(solution)/shard_map/ppermute | solution.py:14
  266.2 0.1 pad_maximum_fusion
  266.3 0.1 fusion.134
  266.4 0.1 reshape.114
  266.5 0.3 copy.35
  266.9 0.1 reshape.112
  267.0 0.3 copy.37
  267.3 77.9 %all-gather.11.cloned.1.call-done = bf16[4096,2048]{1,0:T(8,128)(2,1)} async-done(((bf16[1024,2048]{1,0:T(8,128)(2,1)}), bf16[4096,2048]{1,0:T(8,128)(2,1)}) %all-gather.11.cloned.1.call-update) | async-done | bytes 16777232 | tf_op jit(solution)/shard_map/all_gather | solution.py:57
  345.2 8.2 %convolution_convert_fusion.2 = bf16[128,2048]{1,0:T(8,128)(2,1)S(1)} fusion(bf16[4096,2048]{1,0:T(8,128)(2,1)} %all-gather.11.cloned.1.call-done, bf16[128,4096]{1,0:T(8,128)(2,1)S(1)} %copy-done, f32[128]{0:T(128)S(1)} %add_rsqrt_fusion.1), kind=kOutput, calls=%fused_computation.19 | convolution fusion | flops 2149318656 | bytes 18350592 | tf_op jit(solution)/shard_map/dot_general | solution.py:63
  353.4 1.0 copy.51
  354.4 4.5 fusion.137
  358.9 2.7 fusion.15
  361.6 1.8 fusion.139
  363.4 0.5 fusion.22
  363.9 0.2 copy-done.2
  364.2 0.8 fusion.3
  365.0 1.3 fusion.21
  366.3 1.8 fusion.138
  368.2 0.1 fusion.136
  368.3 0.8 fusion.135
  369.0 1.3 collective-permute-start.3
  370.3 1.3 collective-permute-start.5
  371.6 1.3 collective-permute-start.4
  372.9 1.3 collective-permute-start.6
  374.2 1.5 collective-permute-start.8
  375.7 11.7 %fusion.141 = f32[128,4096]{1,0:T(8,128)S(1)} fusion(bf16[128,2048]{0,1:T(8,128)(2,1)} %bitcast.87, bf16[4096,2048]{1,0:T(8,128)(2,1)} %all-gather.11.cloned.1.call-done), kind=kOutput, calls=%fused_computation.182 | convolution fusion | flops 2147483648 | bytes 19398656 | tf_op jit(solution)/shard_map/tc,dc->td/dot_general | solution.py:141
  387.4 1.3 collective-permute-start.7
  388.8 1.2 fusion.91
  390.0 7.9 %collective-permute-done.7 = bf16[128,4,128]{0,2,1:T(8,128)(2,1)S(1)} collective-permute-done((bf16[128,4,128]{0,2,1:T(8,128)(2,1)S(1)}, bf16[128,4,128]{0,2,1:T(8,128)(2,1)S(1)}, u32[]{:S(2)}, u32[]{:S(2)}) %collective-permute-start.7) | collective-permute-done | bytes 131104 | tf_op jit(solution)/shard_map/ppermute | solution.py:14
  397.9 1.1 fusion.88
  399.0 7.3 %fusion.1 = bf16[128,4096]{1,0:T(8,128)(2,1)} fusion(f32[128,4096]{1,0:T(8,128)S(1)} %fusion.141, bf16[4096,1024]{1,0:T(8,128)(2,1)} %bitcast.80, bf16[128,512]{0,1:T(8,128)(2,1)S(1)} %bitcast.93, bf16[128,512]{0,1:T(8,128)(2,1)S(1)} %bitcast.92), kind=kOutput, calls=%fused_computation.2 | convolution fusion | flops 1075314688 | bytes 11796480 | tf_op jit(solution)/shard_map/tc,dc->td/dot_general | solution.py:142
  406.3 0.0 reduce-scatter.2.cloned.1.call-start
  406.3 40.4 %all-reduce.6.cloned.1.call-done = bf16[128,4096]{1,0:T(8,128)(2,1)} async-done(((bf16[128,4096]{1,0:T(8,128)(2,1)}), bf16[128,4096]{1,0:T(8,128)(2,1)}) %all-reduce.6.cloned.1.call-update) | async-done | bytes 1048592 | tf_op jit(solution)/shard_map/psum | solution.py:145
  446.8 1.8 fusion.9
  448.6 12.3 %convolution_convert_fusion.1 = bf16[128,2560]{1,0:T(8,128)(2,1)S(1)} fusion(bf16[2560,1280]{1,0:T(8,128)(2,1)} %bitcast.83, bf16[1280,4096]{1,0:T(8,128)(2,1)} %all-gather.7.cloned.1.call-done, bf16[128,4096]{1,0:T(8,128)(2,1)S(1)} %copy-done, bf16[128,4096]{1,0:T(8,128)(2,1)S(1)} %copy-done.5, f32[128]{0:T(128)S(1)} %broadcast_multiply_fusion.3, ...), kind=kOutput, calls=%fused_computation.9 | convolution fusion | flops 2186674176 | bytes 20448256 | tf_op jit(solution)/shard_map/th,fh->tf/dot_general | solution.py:150
  460.9 1.2 convert_element_type.119
  462.1 0.1 dynamic-slice.1
  462.2 16.2 %reduce-scatter.2.cloned.1.call-done = bf16[256,640]{1,0:T(8,128)(2,1)} async-done(((bf16[512,640]{1,0:T(8,128)(2,1)}), bf16[256,640]{1,0:T(8,128)(2,1)}) %reduce-scatter.2.cloned.1.call-update) | async-done | bytes 327696 | tf_op jit(solution)/shard_map/reduce_scatter | solution.py:153
  478.4 1.2 convert_reduce_fusion.1
  479.5 1.9 fusion.35
  (40 shorter events, 0.3 us)
Async XLA Ops:
  6.5 53.0 %all-gather.5.cloned.1.call-start = ((), (), s32[]{:S(2)}) async-start(), calls=%async_computation.1 | async-start | bytes 8192000 | tf_op jit(solution)/shard_map/all_gather | solution.py:45
  7.3 1.5 copy-start.3
  7.3 124.0 %all-gather.7.cloned.1.call-start = ((), (), s32[]{:S(2)}) async-start(), calls=%async_computation.2 | async-start | bytes 13107200 | tf_op jit(solution)/shard_map/all_gather | solution.py:49
  8.0 183.1 %all-gather.9.cloned.1.call-start = ((), (), s32[]{:S(2)}) async-start(), calls=%async_computation.4 | async-start | bytes 10485760 | tf_op jit(solution)/shard_map/all_gather | solution.py:58
  8.8 224.7 %all-reduce.4.cloned.1.call-start = ((), (), s32[]{:S(2)}) async-start(), calls=%async_computation.3 | async-start | bytes 2097152 | tf_op jit(solution)/shard_map/psum | solution.py:52
  63.4 75.7 %copy-start.6 = (f32[128,1280]{1,0:T(8,128)}, f32[128,1280]{1,0:T(8,128)S(1)}, u32[]{:S(2)}) copy-start(f32[128,1280]{1,0:T(8,128)S(1)} %fusion.140) | copy-start | bytes 1966084
  139.1 0.7 copy-start.9
  139.1 206.1 %all-gather.11.cloned.1.call-start = ((), (), s32[]{:S(2)}) async-start(), calls=%async_computation.5 | async-start | bytes 20971520 | tf_op jit(solution)/shard_map/all_gather | solution.py:57
  139.7 307.1 %all-reduce.6.cloned.1.call-start = ((), (), s32[]{:S(2)}) async-start(), calls=%async_computation.6 | async-start | bytes 2097152 | tf_op jit(solution)/shard_map/psum | solution.py:145
  235.0 11.9 %copy-start.8 = (bf16[128,2048]{1,0:T(8,128)(2,1)S(1)}, bf16[128,2048]{1,0:T(8,128)(2,1)}, u32[]{:S(2)}) copy-start(bf16[128,2048]{1,0:T(8,128)(2,1)} %param.12) | copy-start | bytes 1572868
  240.1 7.3 %collective-permute-start.2 = (bf16[128,1024]{1,0:T(8,128)(2,1)S(1)}, bf16[128,1024]{1,0:T(8,128)(2,1)S(1)}, u32[]{:S(2)}, u32[]{:S(2)}) collective-permute-start(bf16[128,1024]{1,0:T(8,128)(2,1)S(1)} %convolution_convert_fusion.3), channel_id=1, source_target_pairs={{0,2},{2,4},{4,6},{1,3},{3,5},{5,7},{8,10},{10,12},{12,14},{9,11},... | collective-permute-start | bytes 786440 | tf_op jit(solution)/shard_map/ppermute | solution.py:14
  241.7 15.8 %collective-permute-start.1 = (bf16[128,1024]{1,0:T(8,128)(2,1)S(1)}, bf16[128,1024]{1,0:T(8,128)(2,1)S(1)}, u32[]{:S(2)}, u32[]{:S(2)}) collective-permute-start(bf16[128,1024]{1,0:T(8,128)(2,1)S(1)} %convolution_convert_fusion.3), channel_id=1, source_target_pairs={{0,4},{2,6},{1,5},{3,7},{8,12},{10,14},{9,13},{11,15},{16,20},{18,... | collective-permute-start | bytes 786440 | tf_op jit(solution)/shard_map/ppermute | solution.py:14
  245.4 20.8 %collective-permute-start = (bf16[128,1024]{1,0:T(8,128)(2,1)S(1)}, bf16[128,1024]{1,0:T(8,128)(2,1)S(1)}, u32[]{:S(2)}, u32[]{:S(2)}) collective-permute-start(bf16[128,1024]{1,0:T(8,128)(2,1)S(1)} %convolution_convert_fusion.3), channel_id=1, source_target_pairs={{0,6},{1,7},{8,14},{9,15},{16,22},{17,23},{24,30},{25,31}} | collective-permute-start | bytes 786440 | tf_op jit(solution)/shard_map/ppermute | solution.py:14
  266.4 78.8 %copy-start = (bf16[128,4096]{1,0:T(8,128)(2,1)S(1)}, bf16[128,4096]{1,0:T(8,128)(2,1)}, u32[]{:S(2)}) copy-start(bf16[128,4096]{1,0:T(8,128)(2,1)} %all-reduce.4.cloned.1.call-done) | copy-start | bytes 3145732
  361.6 2.6 copy-start.2
  365.0 1.3 copy-start.4
  369.0 18.4 %collective-permute-start.3 = (bf16[128,4,128]{0,2,1:T(8,128)(2,1)}, bf16[128,4,128]{0,2,1:T(8,128)(2,1)}, u32[]{:S(2)}, u32[]{:S(2)}) collective-permute-start(bf16[128,4,128]{0,2,1:T(8,128)(2,1)} %get-tuple-element.13), channel_id=1, source_target_pairs={{2,0},{4,2},{6,4},{3,1},{5,3},{7,5},{10,8},{12,10},{14,12},{11,9},... | collective-permute-start | bytes 393224 | tf_op jit(solution)/shard_map/ppermute | solution.py:14
  370.3 18.4 %collective-permute-start.5 = (bf16[128,4,128]{0,2,1:T(8,128)(2,1)}, bf16[128,4,128]{0,2,1:T(8,128)(2,1)}, u32[]{:S(2)}, u32[]{:S(2)}) collective-permute-start(bf16[128,4,128]{0,2,1:T(8,128)(2,1)} %get-tuple-element.14), channel_id=1, source_target_pairs={{6,0},{7,1},{14,8},{15,9},{22,16},{23,17},{30,24},{31,25}} | collective-permute-start | bytes 393224 | tf_op jit(solution)/shard_map/ppermute | solution.py:14
  371.6 17.1 %collective-permute-start.4 = (bf16[128,4,128]{0,2,1:T(8,128)(2,1)}, bf16[128,4,128]{0,2,1:T(8,128)(2,1)}, u32[]{:S(2)}, u32[]{:S(2)}) collective-permute-start(bf16[128,4,128]{0,2,1:T(8,128)(2,1)} %get-tuple-element.15), channel_id=1, source_target_pairs={{4,0},{6,2},{5,1},{7,3},{12,8},{14,10},{13,9},{15,11},{20,16},{22,... | collective-permute-start | bytes 393224 | tf_op jit(solution)/shard_map/ppermute | solution.py:14
  372.9 17.0 %collective-permute-start.6 = (bf16[128,4,128]{0,2,1:T(8,128)(2,1)S(1)}, bf16[128,4,128]{0,2,1:T(8,128)(2,1)}, u32[]{:S(2)}, u32[]{:S(2)}) collective-permute-start(bf16[128,4,128]{0,2,1:T(8,128)(2,1)S(1)} %get-tuple-element.16), channel_id=1, source_target_pairs={{2,0},{4,2},{6,4},{3,1},{5,3},{7,5},{10,8},{12,10},{14,12},{11,9},... | collective-permute-start | bytes 393224 | tf_op jit(solution)/shard_map/ppermute | solution.py:14
  374.2 15.7 %collective-permute-start.8 = (bf16[128,4,128]{0,2,1:T(8,128)(2,1)S(1)}, bf16[128,4,128]{0,2,1:T(8,128)(2,1)}, u32[]{:S(2)}, u32[]{:S(2)}) collective-permute-start(bf16[128,4,128]{0,2,1:T(8,128)(2,1)S(1)} %get-tuple-element.17), channel_id=1, source_target_pairs={{6,0},{7,1},{14,8},{15,9},{22,16},{23,17},{30,24},{31,25}} | collective-permute-start | bytes 393224 | tf_op jit(solution)/shard_map/ppermute | solution.py:14
  387.4 10.4 %collective-permute-start.7 = (bf16[128,4,128]{0,2,1:T(8,128)(2,1)S(1)}, bf16[128,4,128]{0,2,1:T(8,128)(2,1)S(1)}, u32[]{:S(2)}, u32[]{:S(2)}) collective-permute-start(bf16[128,4,128]{0,2,1:T(8,128)(2,1)S(1)} %get-tuple-element.18), channel_id=1, source_target_pairs={{4,0},{6,2},{5,1},{7,3},{12,8},{14,10},{13,9},{15,11},{20,16},{22,... | collective-permute-start | bytes 393224 | tf_op jit(solution)/shard_map/ppermute | solution.py:14
  406.2 42.3 %copy-start.7 = (f32[128,1280]{1,0:T(8,128)S(1)}, f32[128,1280]{1,0:T(8,128)}, u32[]{:S(2)}) copy-start(f32[128,1280]{1,0:T(8,128)} %copy-done.6) | copy-start | bytes 1966084
  406.3 72.1 %reduce-scatter.2.cloned.1.call-start = ((), (), s32[]{:S(2)}) async-start(), calls=%async_computation.7 | async-start | bytes 983040 | tf_op jit(solution)/shard_map/reduce_scatter | solution.py:153
  446.8 1.8 copy-start.5
  460.9 17.5 %copy-start.1 = (f32[512,640]{1,0:T(8,128)S(1)}, f32[512,640]{1,0:T(8,128)}, u32[]{:S(2)}) copy-start(f32[512,640]{1,0:T(8,128)} %get-tuple-element.11) | copy-start | bytes 3932164
Sparse Core Ops, SparseCore 0:
  8.9 50.5 all-gather.4
  61.1 70.1 all-gather.6
  132.8 58.2 all-gather.8
  193.3 40.1 all-reduce.3
  234.9 110.2 all-gather.10
  406.4 40.3 all-reduce.5
  462.3 16.0 reduce-scatter.1
where the time goes:
time: 489 us; the launch traced here: 488 us
  waiting for transfers between devices  365 us (75%)
  matrix products  66.9 us (14%)
  starting transfers between devices  15 us (3%)
  local copies, waits for them, and re-layouts  14.4 us (3%)
  between operations  13.9 us (3%)
  other arithmetic  13.4 us (3%)
    all_gather x1, waiting for transfers between devices, local(): lax.all_gather(w_query, 'seq', axis=0, tiled=True)  77.9 us
    all_gather x1, waiting for transfers between devices, local(): second_tile = lax.all_gather(w_merge2, 'seq', axis=1, tiled=True)  67.9 us
    all_gather x1, waiting for transfers between devices, local(): lax.all_gather(w_keyval, 'seq', axis=0, tiled=True)  51.3 us
    all_gather x1, waiting for transfers between devices, local(): first_tile = lax.all_gather(w_merge1, 'seq', axis=1, tiled=True)  48.7 us
    psum x1, waiting for transfers between devices, local(): lax.psum(dnormed_part.astype(jnp.bfloat16), 'mp').astype(jnp.float32)  40.4 us
    psum x1, waiting for transfers between devices, local(): merged = lax.psum(partial_value.astype(jnp.bfloat16), 'mp')  33 us
    ppermute x9, waiting for transfers between devices, shifted_2(): lax.ppermute(value, axis, [(source, source + steps) for source in range(i...  26.7 us
    reduce_scatter x1, waiting for transfers between devices, local(): lax.psum_scatter(dmerge_part.reshape(patch_rows, feat_width).astype(jnp.b...  16.2 us
  transfers between devices with their start and end apart: 16, of which 10 were waited for; matrix products, arithmetic and copies ran while one was open for 9% of the time, Pallas kernels for 0%

commit v1 on v0

--- a/solution.py
+++ b/solution.py
@@ -46,7 +46,9 @@
     first_flat = first_tile.reshape(4 * feat_width, first_tile.shape[2])
     hidden_pre = jnp.dot(merge_in, first_flat, preferred_element_type=jnp.float32)
     hidden = jax.nn.gelu(hidden_pre, approximate=False).astype(jnp.bfloat16)
-    second_tile = lax.all_gather(w_merge2, "seq", axis=1, tiled=True)
+    second_tile = jnp.concatenate(
+        lax.all_to_all(jnp.stack([w_merge2] * lax.axis_size("seq")), "seq", 0, 0), axis=1
+    )
     model_width = second_tile.shape[1]
     partial_value = jnp.dot(hidden, second_tile, preferred_element_type=jnp.float32)
     merged = lax.psum(partial_value.astype(jnp.bfloat16), "mp")

time: 489 us -> 537 us (1.098)
  waiting for transfers between devices: 365 us -> 399 us
  local copies, waits for them, and re-layouts: 14.4 us -> 23.2 us
    all_to_all x0 -> x1, waiting for transfers between devices: none -> 74.4 us  [local(): lax.all_to_all(jnp.stack([w_merge2] * lax.axis_size('seq')), 'seq', 0, 0)]
    all_gather x1 -> x0, waiting for transfers between devices: 67.9 us -> none  [local(): second_tile = lax.all_gather(w_merge2, 'seq', axis=1, tiled=True)]
    all_gather x1, waiting for transfers between devices: 48.7 us -> 68.6 us  [local(): first_tile = lax.all_gather(w_merge1, 'seq', axis=1, tiled=True)]
    all_gather x1, waiting for transfers between devices: 77.9 us -> 70.3 us  [local(): lax.all_gather(w_query, 'seq', axis=0, tiled=True)]
    all_gather x1, waiting for transfers between devices: 51.3 us -> 58.3 us  [local(): lax.all_gather(w_keyval, 'seq', axis=0, tiled=True)]
    all_to_all x0 -> x1, starting transfers between devices: none -> 6.42 us  [local(): lax.all_to_all(jnp.stack([w_merge2] * lax.axis_size('seq')), 'seq', 0, 0)]
    psum x1, waiting for transfers between devices: 33 us -> 38.8 us  [local(): merged = lax.psum(partial_value.astype(jnp.bfloat16), 'mp')]
    unnamed x23 -> x24, local copies, waits for them, and re-layouts: 10 us -> 14.1 us
where the time goes in v1:
time: 537 us; the launch traced here: 536 us
  waiting for transfers between devices  399 us (74%)
  matrix products  67 us (12%)
  local copies, waits for them, and re-layouts  23.2 us (4%)
  starting transfers between devices  19.7 us (4%)
  between operations  13.9 us (3%)
  other arithmetic  13.4 us (2%)
    all_to_all x1, waiting for transfers between devices, local(): lax.all_to_all(jnp.stack([w_merge2] * lax.axis_size('seq')), 'seq', 0, 0)  74.4 us
    all_gather x1, waiting for transfers between devices, local(): lax.all_gather(w_query, 'seq', axis=0, tiled=True)  70.3 us
    all_gather x1, waiting for transfers between devices, local(): first_tile = lax.all_gather(w_merge1, 'seq', axis=1, tiled=True)  68.6 us
    all_gather x1, waiting for transfers between devices, local(): lax.all_gather(w_keyval, 'seq', axis=0, tiled=True)  58.3 us
    psum x1, waiting for transfers between devices, local(): lax.psum(dnormed_part.astype(jnp.bfloat16), 'mp').astype(jnp.float32)  41.6 us
    psum x1, waiting for transfers between devices, local(): merged = lax.psum(partial_value.astype(jnp.bfloat16), 'mp')  38.8 us
    ppermute x9, waiting for transfers between devices, shifted_2(): lax.ppermute(value, axis, [(source, source + steps) for source in range(i...  28.7 us
    reduce_scatter x1, waiting for transfers between devices, local(): lax.psum_scatter(dmerge_part.reshape(patch_rows, feat_width).astype(jnp.b...  16.2 us
  transfers between devices with their start and end apart: 16, of which 10 were waited for; matrix products, arithmetic and copies ran while one was open for 9% of the time, Pallas kernels for 0%

profile of v1, /device:TPU:0, one launch (start us, length us, event | category | flops | bytes accessed | tf_op | source)
XLA Modules:
  0.0 535.8 jit_solution(3851465798084823030)
XLA Ops:
  6.5 0.7 all-gather.4.cloned.1.call-update
  7.3 3.0 copy.33
  10.2 4.7 stack.2
  14.9 6.4 %all-to-all-start = ((bf16[4,1280,1024]{1,2,0:T(8,128)(2,1)}), bf16[4,1280,1024]{1,2,0:T(8,128)(2,1)}, u32[]{:S(2)}, u32[]{:S(2)}) async-start(bf16[4,1280,1024]{1,2,0:T(8,128)(2,1)} %stack.2), calls=%async_computation | async-start | bytes 20971520 | tf_op jit(solution)/shard_map/all_to_all | solution.py:50
  21.4 0.3 convert_reduce_fusion
  21.7 1.3 fusion.20
  23.0 0.4 reshape.117
  23.4 68.6 %all-gather.4.cloned.1.call-done = bf16[4,640,1280]{2,1,0:T(8,128)(2,1)} async-done(((bf16[4,160,1280]{2,1,0:T(8,128)(2,1)}), bf16[4,640,1280]{2,1,0:T(8,128)(2,1)}) %all-gather.4.cloned.1.call-update) | async-done | bytes 6553616 | tf_op jit(solution)/shard_map/all_gather | solution.py:45
  92.0 3.9 fusion.140
  95.9 74.4 %all-to-all-done = bf16[4,1280,1024]{1,2,0:T(8,128)(2,1)} async-done(((bf16[4,1280,1024]{1,2,0:T(8,128)(2,1)}), bf16[4,1280,1024]{1,2,0:T(8,128)(2,1)}, u32[]{:S(2)}, u32[]{:S(2)}) %all-to-all-start) | async-done | bytes 10485792 | tf_op jit(solution)/shard_map/all_to_all | solution.py:50
  170.2 9.4 %convolution_convert_fusion = bf16[128,4096]{1,0:T(8,128)(2,1)} fusion(bf16[1280,4096]{0,1:T(8,128)(2,1)} %bitcast.2, f32[128,1280]{1,0:T(8,128)S(1)} %fusion.140), kind=kOutput, calls=%fused_computation.3 | convolution fusion | flops 1353351168 | bytes 12189696 | tf_op jit(solution)/shard_map/dot_general | solution.py:53
  179.7 0.7 all-gather.6.cloned.1.call-update
  180.4 0.5 all-gather.8.cloned.1.call-update
  181.1 0.1 pad_dynamic-slice_fusion
  181.1 38.8 %all-reduce.4.cloned.1.call-done = bf16[128,4096]{1,0:T(8,128)(2,1)} async-done(((bf16[128,4096]{1,0:T(8,128)(2,1)}), bf16[128,4096]{1,0:T(8,128)(2,1)}) %all-reduce.4.cloned.1.call-update) | async-done | bytes 1048592 | tf_op jit(solution)/shard_map/psum | solution.py:54
  219.9 1.5 fusion.8
  221.4 58.3 %all-gather.6.cloned.1.call-done = bf16[4096,2,512]{2,1,0:T(2,128)(2,1)} async-done(((bf16[1024,2,512]{2,1,0:T(2,128)(2,1)}), bf16[4096,2,512]{2,1,0:T(2,128)(2,1)}) %all-gather.6.cloned.1.call-update) | async-done | bytes 8388624 | tf_op jit(solution)/shard_map/all_gather | solution.py:60
  279.8 10.4 %copy.66 = bf16[512,8,2,512]{3,1,2,0:T(8,128)(2,1)} copy(bf16[512,8,2,512]{3,2,1,0:T(2,128)(2,1)} %bitcast.84) | data formatting | bytes 16777216
  290.2 6.2 %convolution_convert_fusion.3 = bf16[128,1024]{1,0:T(8,128)(2,1)S(1)} fusion(bf16[4096,1024]{1,0:T(8,128)(2,1)} %bitcast.82, bf16[128,4096]{1,0:T(8,128)(2,1)S(1)} %copy-done, f32[128]{0:T(128)S(1)} %add_rsqrt_fusion.1), kind=kOutput, calls=%fused_computation.43 | convolution fusion | flops 1075445760 | bytes 9699840 | tf_op jit(solution)/shard_map/dot_general | solution.py:68
  296.4 2.1 collective-permute-start.2
  298.5 1.5 collective-permute-start.1
  300.0 1.5 collective-permute-start
  301.5 0.3 copy.36
  301.8 0.2 compare_and_fusion
  302.0 10.2 %collective-permute-done.1 = bf16[128,1024]{1,0:T(8,128)(2,1)S(1)} collective-permute-done((bf16[128,1024]{1,0:T(8,128)(2,1)S(1)}, bf16[128,1024]{1,0:T(8,128)(2,1)S(1)}, u32[]{:S(2)}, u32[]{:S(2)}) %collective-permute-start.1) | collective-permute-done | bytes 262176 | tf_op jit(solution)/shard_map/ppermute | solution.py:14
  312.3 10.6 %collective-permute-done = bf16[128,1024]{1,0:T(8,128)(2,1)S(1)} collective-permute-done((bf16[128,1024]{1,0:T(8,128)(2,1)S(1)}, bf16[128,1024]{1,0:T(8,128)(2,1)S(1)}, u32[]{:S(2)}, u32[]{:S(2)}) %collective-permute-start) | collective-permute-done | bytes 262176 | tf_op jit(solution)/shard_map/ppermute | solution.py:14
  322.9 0.1 pad_maximum_fusion
  322.9 0.1 fusion.134
  323.0 0.1 reshape.124
  323.1 0.3 copy.49
  323.5 0.1 reshape.122
  323.6 0.3 copy.51
  323.9 70.3 %all-gather.8.cloned.1.call-done = bf16[4096,2048]{1,0:T(8,128)(2,1)} async-done(((bf16[1024,2048]{1,0:T(8,128)(2,1)}), bf16[4096,2048]{1,0:T(8,128)(2,1)}) %all-gather.8.cloned.1.call-update) | async-done | bytes 16777232 | tf_op jit(solution)/shard_map/all_gather | solution.py:59
  394.2 8.1 %convolution_convert_fusion.2 = bf16[128,2048]{1,0:T(8,128)(2,1)S(1)} fusion(bf16[4096,2048]{1,0:T(8,128)(2,1)} %all-gather.8.cloned.1.call-done, bf16[128,4096]{1,0:T(8,128)(2,1)S(1)} %copy-done, f32[128]{0:T(128)S(1)} %add_rsqrt_fusion.1), kind=kOutput, calls=%fused_computation.19 | convolution fusion | flops 2149318656 | bytes 18350592 | tf_op jit(solution)/shard_map/dot_general | solution.py:65
  402.3 1.0 copy.65
  403.4 4.5 fusion.137
  407.9 2.7 fusion.15
  410.6 1.8 fusion.139
  412.4 0.5 fusion.22
  412.9 0.2 copy-done.2
  413.1 0.8 fusion.3
  414.0 1.3 fusion.21
  415.3 1.8 fusion.138
  417.1 0.1 fusion.136
  417.2 0.8 fusion.135
  418.0 1.3 collective-permute-start.3
  419.3 1.3 collective-permute-start.5
  420.6 1.3 collective-permute-start.4
  421.9 1.3 collective-permute-start.6
  423.2 1.5 collective-permute-start.8
  424.7 11.7 %fusion.141 = f32[128,4096]{1,0:T(8,128)S(1)} fusion(bf16[128,2048]{0,1:T(8,128)(2,1)} %bitcast.90, bf16[4096,2048]{1,0:T(8,128)(2,1)} %all-gather.8.cloned.1.call-done), kind=kOutput, calls=%fused_computation.182 | convolution fusion | flops 2147483648 | bytes 19398656 | tf_op jit(solution)/shard_map/tc,dc->td/dot_general | solution.py:143
  436.4 1.3 collective-permute-start.7
  437.7 1.2 fusion.91
  438.9 7.9 %collective-permute-done.7 = bf16[128,4,128]{0,2,1:T(8,128)(2,1)S(1)} collective-permute-done((bf16[128,4,128]{0,2,1:T(8,128)(2,1)S(1)}, bf16[128,4,128]{0,2,1:T(8,128)(2,1)S(1)}, u32[]{:S(2)}, u32[]{:S(2)}) %collective-permute-start.7) | collective-permute-done | bytes 131104 | tf_op jit(solution)/shard_map/ppermute | solution.py:14
  446.8 1.1 fusion.88
  448.0 7.3 %fusion.1 = bf16[128,4096]{1,0:T(8,128)(2,1)} fusion(f32[128,4096]{1,0:T(8,128)S(1)} %fusion.141, bf16[4096,1024]{1,0:T(8,128)(2,1)} %bitcast.83, bf16[128,512]{0,1:T(8,128)(2,1)S(1)} %bitcast.96, bf16[128,512]{0,1:T(8,128)(2,1)S(1)} %bitcast.95), kind=kOutput, calls=%fused_computation.2 | convolution fusion | flops 1075314688 | bytes 11796480 | tf_op jit(solution)/shard_map/tc,dc->td/dot_general | solution.py:144
  455.3 41.6 %all-reduce.6.cloned.1.call-done = bf16[128,4096]{1,0:T(8,128)(2,1)} async-done(((bf16[128,4096]{1,0:T(8,128)(2,1)}), bf16[128,4096]{1,0:T(8,128)(2,1)}) %all-reduce.6.cloned.1.call-update) | async-done | bytes 1048592 | tf_op jit(solution)/shard_map/psum | solution.py:147
  496.9 1.8 fusion.9
  498.7 9.7 %convolution_convert_fusion.1 = bf16[128,2560]{1,0:T(8,128)(2,1)S(1)} fusion(bf16[2560,1280]{1,0:T(8,128)(2,1)} %bitcast.86, bf16[1280,4096]{0,1:T(8,128)(2,1)} %bitcast.2, bf16[128,4096]{1,0:T(8,128)(2,1)S(1)} %copy-done, bf16[128,4096]{1,0:T(8,128)(2,1)S(1)} %copy-done.5, f32[128]{0:T(128)S(1)} %broadcast_multiply_fusion.3, f32[128]{0:T(128)S(1)} %add_rsqrt_fusion.1, ...), kind=kOutput, calls=%fused_computation.9 | convolution fusion | flops 2186674176 | bytes 20448256 | tf_op jit(solution)/shard_map/th,fh->tf/dot_general | solution.py:152
  508.4 1.2 convert_element_type.119
  509.7 0.1 dynamic-slice.1
  509.7 16.2 %reduce-scatter.2.cloned.1.call-done = bf16[256,640]{1,0:T(8,128)(2,1)} async-done(((bf16[512,640]{1,0:T(8,128)(2,1)}), bf16[256,640]{1,0:T(8,128)(2,1)}) %reduce-scatter.2.cloned.1.call-update) | async-done | bytes 327696 | tf_op jit(solution)/shard_map/reduce_scatter | solution.py:155
  525.9 1.2 convert_reduce_fusion.1
  527.1 1.9 fusion.35
  (41 shorter events, 0.4 us)
Async XLA Ops:
  6.5 85.5 %all-gather.4.cloned.1.call-start = ((), (), s32[]{:S(2)}) async-start(), calls=%async_computation.2 | async-start | bytes 8192000 | tf_op jit(solution)/shard_map/all_gather | solution.py:45
  14.9 6.5 %copy-start.3 = (bf16[512,640]{1,0:T(8,128)(2,1)S(1)}, bf16[512,640]{1,0:T(8,128)(2,1)}, u32[]{:S(2)}) copy-start(bf16[512,640]{1,0:T(8,128)(2,1)} %param.7) | copy-start | bytes 1966084
  14.9 155.3 %all-to-all-start = ((bf16[4,1280,1024]{1,2,0:T(8,128)(2,1)}), bf16[4,1280,1024]{1,2,0:T(8,128)(2,1)}, u32[]{:S(2)}, u32[]{:S(2)}) async-start(bf16[4,1280,1024]{1,2,0:T(8,128)(2,1)} %stack.2), calls=%async_computation | async-start | bytes 20971520 | tf_op jit(solution)/shard_map/all_to_all | solution.py:50
  21.3 198.5 %all-reduce.4.cloned.1.call-start = ((), (), s32[]{:S(2)}) async-start(), calls=%async_computation.3 | async-start | bytes 2097152 | tf_op jit(solution)/shard_map/psum | solution.py:54
  95.9 83.7 %copy-start.6 = (f32[128,1280]{1,0:T(8,128)}, f32[128,1280]{1,0:T(8,128)S(1)}, u32[]{:S(2)}) copy-start(f32[128,1280]{1,0:T(8,128)S(1)} %fusion.140) | copy-start | bytes 1966084
  179.6 100.1 %all-gather.6.cloned.1.call-start = ((), (), s32[]{:S(2)}) async-start(), calls=%async_computation.4 | async-start | bytes 10485760 | tf_op jit(solution)/shard_map/all_gather | solution.py:60
  180.4 0.7 copy-start.9
  180.4 213.8 %all-gather.8.cloned.1.call-start = ((), (), s32[]{:S(2)}) async-start(), calls=%async_computation.5 | async-start | bytes 20971520 | tf_op jit(solution)/shard_map/all_gather | solution.py:59
  181.0 315.9 %all-reduce.6.cloned.1.call-start = ((), (), s32[]{:S(2)}) async-start(), calls=%async_computation.6 | async-start | bytes 2097152 | tf_op jit(solution)/shard_map/psum | solution.py:147
  279.8 10.4 %copy-start = (bf16[128,4096]{1,0:T(8,128)(2,1)S(1)}, bf16[128,4096]{1,0:T(8,128)(2,1)}, u32[]{:S(2)}) copy-start(bf16[128,4096]{1,0:T(8,128)(2,1)} %all-reduce.4.cloned.1.call-done) | copy-start | bytes 3145732
  290.2 11.3 %copy-start.8 = (bf16[128,2048]{1,0:T(8,128)(2,1)S(1)}, bf16[128,2048]{1,0:T(8,128)(2,1)}, u32[]{:S(2)}) copy-start(bf16[128,2048]{1,0:T(8,128)(2,1)} %param.12) | copy-start | bytes 1572868
  296.4 5.6 %collective-permute-start.2 = (bf16[128,1024]{1,0:T(8,128)(2,1)S(1)}, bf16[128,1024]{1,0:T(8,128)(2,1)S(1)}, u32[]{:S(2)}, u32[]{:S(2)}) collective-permute-start(bf16[128,1024]{1,0:T(8,128)(2,1)S(1)} %convolution_convert_fusion.3), channel_id=1, source_target_pairs={{0,2},{2,4},{4,6},{1,3},{3,5},{5,7},{8,10},{10,12},{12,14},{9,11},... | collective-permute-start | bytes 786440 | tf_op jit(solution)/shard_map/ppermute | solution.py:14
  298.5 13.8 %collective-permute-start.1 = (bf16[128,1024]{1,0:T(8,128)(2,1)S(1)}, bf16[128,1024]{1,0:T(8,128)(2,1)S(1)}, u32[]{:S(2)}, u32[]{:S(2)}) collective-permute-start(bf16[128,1024]{1,0:T(8,128)(2,1)S(1)} %convolution_convert_fusion.3), channel_id=1, source_target_pairs={{0,4},{2,6},{1,5},{3,7},{8,12},{10,14},{9,13},{11,15},{16,20},{18,... | collective-permute-start | bytes 786440 | tf_op jit(solution)/shard_map/ppermute | solution.py:14
  300.0 22.8 %collective-permute-start = (bf16[128,1024]{1,0:T(8,128)(2,1)S(1)}, bf16[128,1024]{1,0:T(8,128)(2,1)S(1)}, u32[]{:S(2)}, u32[]{:S(2)}) collective-permute-start(bf16[128,1024]{1,0:T(8,128)(2,1)S(1)} %convolution_convert_fusion.3), channel_id=1, source_target_pairs={{0,6},{1,7},{8,14},{9,15},{16,22},{17,23},{24,30},{25,31}} | collective-permute-start | bytes 786440 | tf_op jit(solution)/shard_map/ppermute | solution.py:14
  410.6 2.6 copy-start.2
  414.0 1.3 copy-start.4
  418.0 18.4 %collective-permute-start.3 = (bf16[128,4,128]{0,2,1:T(8,128)(2,1)}, bf16[128,4,128]{0,2,1:T(8,128)(2,1)}, u32[]{:S(2)}, u32[]{:S(2)}) collective-permute-start(bf16[128,4,128]{0,2,1:T(8,128)(2,1)} %get-tuple-element.13), channel_id=1, source_target_pairs={{2,0},{4,2},{6,4},{3,1},{5,3},{7,5},{10,8},{12,10},{14,12},{11,9},... | collective-permute-start | bytes 393224 | tf_op jit(solution)/shard_map/ppermute | solution.py:14
  419.3 18.4 %collective-permute-start.5 = (bf16[128,4,128]{0,2,1:T(8,128)(2,1)}, bf16[128,4,128]{0,2,1:T(8,128)(2,1)}, u32[]{:S(2)}, u32[]{:S(2)}) collective-permute-start(bf16[128,4,128]{0,2,1:T(8,128)(2,1)} %get-tuple-element.14), channel_id=1, source_target_pairs={{6,0},{7,1},{14,8},{15,9},{22,16},{23,17},{30,24},{31,25}} | collective-permute-start | bytes 393224 | tf_op jit(solution)/shard_map/ppermute | solution.py:14
  420.6 17.1 %collective-permute-start.4 = (bf16[128,4,128]{0,2,1:T(8,128)(2,1)}, bf16[128,4,128]{0,2,1:T(8,128)(2,1)}, u32[]{:S(2)}, u32[]{:S(2)}) collective-permute-start(bf16[128,4,128]{0,2,1:T(8,128)(2,1)} %get-tuple-element.15), channel_id=1, source_target_pairs={{4,0},{6,2},{5,1},{7,3},{12,8},{14,10},{13,9},{15,11},{20,16},{22,... | collective-permute-start | bytes 393224 | tf_op jit(solution)/shard_map/ppermute | solution.py:14
  421.9 17.0 %collective-permute-start.6 = (bf16[128,4,128]{0,2,1:T(8,128)(2,1)S(1)}, bf16[128,4,128]{0,2,1:T(8,128)(2,1)}, u32[]{:S(2)}, u32[]{:S(2)}) collective-permute-start(bf16[128,4,128]{0,2,1:T(8,128)(2,1)S(1)} %get-tuple-element.16), channel_id=1, source_target_pairs={{2,0},{4,2},{6,4},{3,1},{5,3},{7,5},{10,8},{12,10},{14,12},{11,9},... | collective-permute-start | bytes 393224 | tf_op jit(solution)/shard_map/ppermute | solution.py:14
  423.2 15.7 %collective-permute-start.8 = (bf16[128,4,128]{0,2,1:T(8,128)(2,1)S(1)}, bf16[128,4,128]{0,2,1:T(8,128)(2,1)}, u32[]{:S(2)}, u32[]{:S(2)}) collective-permute-start(bf16[128,4,128]{0,2,1:T(8,128)(2,1)S(1)} %get-tuple-element.17), channel_id=1, source_target_pairs={{6,0},{7,1},{14,8},{15,9},{22,16},{23,17},{30,24},{31,25}} | collective-permute-start | bytes 393224 | tf_op jit(solution)/shard_map/ppermute | solution.py:14
  436.4 10.4 %collective-permute-start.7 = (bf16[128,4,128]{0,2,1:T(8,128)(2,1)S(1)}, bf16[128,4,128]{0,2,1:T(8,128)(2,1)S(1)}, u32[]{:S(2)}, u32[]{:S(2)}) collective-permute-start(bf16[128,4,128]{0,2,1:T(8,128)(2,1)S(1)} %get-tuple-element.18), channel_id=1, source_target_pairs={{4,0},{6,2},{5,1},{7,3},{12,8},{14,10},{13,9},{15,11},{20,16},{22,... | collective-permute-start | bytes 393224 | tf_op jit(solution)/shard_map/ppermute | solution.py:14
  455.2 43.5 %copy-start.7 = (f32[128,1280]{1,0:T(8,128)S(1)}, f32[128,1280]{1,0:T(8,128)}, u32[]{:S(2)}) copy-start(f32[128,1280]{1,0:T(8,128)} %copy-done.6) | copy-start | bytes 1966084
  455.2 70.6 %reduce-scatter.2.cloned.1.call-start = ((), (), s32[]{:S(2)}) async-start(), calls=%async_computation.7 | async-start | bytes 983040 | tf_op jit(solution)/shard_map/reduce_scatter | solution.py:155
  496.9 1.8 copy-start.5
  508.4 17.5 %copy-start.1 = (f32[512,640]{1,0:T(8,128)S(1)}, f32[512,640]{1,0:T(8,128)}, u32[]{:S(2)}) copy-start(f32[512,640]{1,0:T(8,128)} %get-tuple-element.11) | copy-start | bytes 3932164
Sparse Core Ops, SparseCore 0:
  8.9 83.0 all-gather.3
  179.8 40.0 all-reduce.3
  221.5 58.2 all-gather.5
  281.2 112.9 all-gather.7
  455.4 41.4 all-reduce.5
  509.8 16.0 reduce-scatter.1
